TPU v7x, 32 devices: a whole 2x2x4 slice. The times are simulated.
32 devices in a mesh: rows: 8 (over y, x, core), rep: 4 (over z).
Axes of the slice: x: 2, y: 2, z: 4, core: 2. Of those that a mesh axis runs over, the one named last changes fastest.
Arguments:
- maps: float32 [4, 4096, 4096], P('rep', 'rows'), may hold values from -12 to 12
- mask: int32 [4096, 4096], P('rows'), may hold values 0 or 1
- bins: int32 [4096, 4096], P(None, 'rows'), may hold values from 0 to 1023
Outputs:
- spectra: float32 [2, 3, 1024], replicated
All inputs are finite; a program needn't handle non-finite values. No bound on the sum of `mask` on one device may be relied on, other than what follows from the above.
Results may differ from a plain program's by a relative error of at most 0.0016.
Values sent between devices are 32-bit elements; how exact they have to be, the bound alone decides.
No kernel may reach another device: no remote copies, remote signals or barrier semaphores. Data moves between devices by JAX's collectives and lax.ppermute only.
A program may use at most 128 MiB of HBM per device.

v0:
```python
import math
import jax
import jax.numpy as jnp
from jax import lax
from jax.sharding import PartitionSpec as P

NBINS = 1024
precise = lax.Precision.HIGHEST


def partner(array, axis, distance):
    return lax.ppermute(array, axis, [(i, i ^ 1 << distance) for i in range(lax.axis_size(axis))])


def dft_table(count_a, count_b, period):
    first = lax.iota(jnp.int32, count_a)[:, None]
    second = lax.iota(jnp.int32, count_b)[None, :]
    angles = (first * second % period).astype(jnp.float32) * (2.0 * math.pi / period)
    return (jnp.cos(angles), -jnp.sin(angles))


def split_length(length):
    outer_len = 2 ** ((length.bit_length() - 1) // 2)
    return (outer_len, length // outer_len)


def complex_apply(form, real_part, imag_part, table_cos, table_sin):

    def product(left, right):
        return jnp.einsum(form, left, right, precision=precise)

    return (
        product(real_part, table_cos) - product(imag_part, table_sin),
        product(real_part, table_sin) + product(imag_part, table_cos),
    )


def twiddled(real_part, imag_part, table_cos, table_sin):
    return (
        real_part * table_cos - imag_part * table_sin,
        real_part * table_sin + imag_part * table_cos,
    )


def row_transform(values):
    count, length = values.shape
    outer_len, inner_len = split_length(length)
    outer_cos, outer_sin = dft_table(outer_len, outer_len, outer_len)
    inner_cos, inner_sin = dft_table(inner_len, inner_len, inner_len)
    turn_cos, turn_sin = dft_table(outer_len, inner_len, length)
    shaped = values.reshape(count, outer_len, inner_len)
    first_real = jnp.einsum("yan,ak->ykn", shaped, outer_cos, precision=precise)
    first_imag = jnp.einsum("yan,ak->ykn", shaped, outer_sin, precision=precise)
    mid_real, mid_imag = twiddled(first_real, first_imag, turn_cos, turn_sin)
    last_real, last_imag = complex_apply("ykn,nm->ymk", mid_real, mid_imag, inner_cos, inner_sin)
    return (last_real.reshape(count, length), last_imag.reshape(count, length))


def column_transform(pieces):
    real_part, imag_part = pieces
    length, groups, width = real_part.shape
    outer_len, inner_len = split_length(length)
    outer_cos, outer_sin = dft_table(outer_len, outer_len, outer_len)
    inner_cos, inner_sin = dft_table(inner_len, inner_len, inner_len)
    turn_cos, turn_sin = dft_table(outer_len, inner_len, length)
    shaped_real = real_part.reshape(outer_len, inner_len, groups, width)
    shaped_imag = imag_part.reshape(outer_len, inner_len, groups, width)
    first_real, first_imag = complex_apply(
        "anbc,ak->knbc", shaped_real, shaped_imag, outer_cos, outer_sin
    )
    mid_real, mid_imag = twiddled(
        first_real, first_imag, turn_cos[:, :, None, None], turn_sin[:, :, None, None]
    )
    last_real, last_imag = complex_apply("knbc,nm->mkbc", mid_real, mid_imag, inner_cos, inner_sin)
    return (last_real.reshape(length, groups, width), last_imag.reshape(length, groups, width))


def signed_float(indices, extent):
    return jnp.where(indices >= extent // 2, indices - extent, indices).astype(jnp.float32)


def band_terms(fields, freq_y, freq_x, bin_block, nbins_count, extent):
    q_real, q_imag, u_real, u_imag = fields
    radius = jnp.maximum(freq_x * freq_x + freq_y * freq_y, 1.0)
    cos_twice = (freq_x * freq_x - freq_y * freq_y) / radius
    sin_twice = 2.0 * freq_x * freq_y / radius
    e_real = cos_twice * q_real + sin_twice * u_real
    e_imag = cos_twice * q_imag + sin_twice * u_imag
    b_real = -sin_twice * q_real + cos_twice * u_real
    b_imag = -sin_twice * q_imag + cos_twice * u_imag
    inv_area = 1.0 / (extent * extent)
    powers = jnp.stack(
        [
            (e_real * e_real + e_imag * e_imag) * inv_area,
            (b_real * b_real + b_imag * b_imag) * inv_area,
            (e_real * b_real + e_imag * b_imag) * inv_area,
        ]
    ).astype(jnp.bfloat16)
    bit_count = nbins_count.bit_length() - 1
    high_count = 2 ** max(bit_count // 2 - 1, 0)
    low_count = nbins_count // high_count
    high_part = bin_block // low_count
    low_part = bin_block % low_count
    high_hot = (high_part[None] == lax.iota(jnp.int32, high_count)[:, None, None]).astype(
        jnp.bfloat16
    )
    weighted = (powers[:, None] * high_hot[None]).reshape(3 * high_count, -1)
    low_hot = (low_part[None] == lax.iota(jnp.int32, low_count)[:, None, None]).astype(jnp.bfloat16)
    low_hot = low_hot.reshape(low_count, -1)
    sums = lax.dot_general(
        weighted, low_hot, (((1,), (1,)), ((), ())), preferred_element_type=jnp.float32
    )
    return sums.reshape(3, nbins_count)


def on_device(maps, mask, bins):
    extent = bins.shape[0]
    columns = bins.shape[1]
    count = maps.shape[1]
    slab_index = lax.axis_index("rows")
    member = lax.axis_index("rep")
    pair_bit = member % 2
    field = maps[0] * mask.astype(jnp.float32)
    row_real, row_imag = row_transform(field)
    half_rows = extent // 2
    slabs = (
        row_real.reshape(count, extent // columns, columns),
        row_imag.reshape(count, extent // columns, columns),
    )
    spec_real, spec_imag = column_transform(
        (
            lax.all_to_all(slabs[0], "rows", split_axis=1, concat_axis=0, tiled=True),
            lax.all_to_all(slabs[1], "rows", split_axis=1, concat_axis=0, tiled=True),
        )
    )
    spec_real = spec_real.reshape(extent, columns)
    spec_imag = spec_imag.reshape(extent, columns)
    kept_real = lax.dynamic_slice_in_dim(spec_real, pair_bit * half_rows, half_rows, 0)
    kept_imag = lax.dynamic_slice_in_dim(spec_imag, pair_bit * half_rows, half_rows, 0)
    sent_real = lax.dynamic_slice_in_dim(spec_real, (1 - pair_bit) * half_rows, half_rows, 0)
    sent_imag = lax.dynamic_slice_in_dim(spec_imag, (1 - pair_bit) * half_rows, half_rows, 0)
    got_real, got_imag = partner((sent_real, sent_imag), "rep", 0)
    is_first = pair_bit == 0
    fields = (
        jnp.where(is_first, kept_real, got_real),
        jnp.where(is_first, kept_imag, got_imag),
        jnp.where(is_first, got_real, kept_real),
        jnp.where(is_first, got_imag, kept_imag),
    )
    own_bins = lax.dynamic_slice_in_dim(bins, pair_bit * half_rows, half_rows, 0)

    def frequency_of(offset, height):
        rows_here = lax.iota(jnp.int32, height)[:, None] + offset + pair_bit * half_rows
        cols_here = lax.iota(jnp.int32, columns)[None, :] + slab_index * columns
        return (rows_here, cols_here)

    block = min(256, half_rows)
    blocks = half_rows // block
    stacked = tuple((part.reshape(blocks, block, columns) for part in fields))
    bin_blocks = own_bins.reshape(blocks, block, columns)

    def accumulate(running, items):
        block_index, parts, bin_block = items
        rows_here, cols_here = frequency_of(block_index * block, block)
        term = band_terms(
            parts,
            signed_float(rows_here, extent),
            signed_float(cols_here, extent),
            bin_block,
            NBINS,
            extent,
        )
        return (running + term, None)

    partial_sums, _ = lax.scan(
        accumulate,
        jnp.zeros((3, NBINS), jnp.float32),
        (lax.iota(jnp.int32, blocks), stacked, bin_blocks),
    )
    sims_count = lax.axis_size("rep") // 2
    slot = (lax.iota(jnp.int32, sims_count) == member // 2).astype(jnp.float32)[:, None, None]
    totals = lax.psum(slot * partial_sums[None], ("rows", "rep"))
    auto = NBINS / (extent * extent)
    cross = math.sqrt(auto)
    factors = jnp.array([auto, auto, cross], jnp.float32)[None, :, None]
    return totals * factors


def solution(mesh):
    in_specs = (P("rep", "rows", None), P("rows", None), P(None, "rows"))
    out_specs = P()
    return jax.shard_map(
        on_device, mesh=mesh, in_specs=in_specs, out_specs=out_specs, check_vma=False
    )
```

profile of v0, /device:TPU:0, one launch (start us, length us, event | category | flops | bytes accessed | tf_op | source)
XLA Modules:
  0.0 1004.3 jit_solution(9013043201485757183)
XLA Ops:
  18.2 11.1 %bitcast_multiply_fusion = f32[512,4096]{0,1:T(8,128)} fusion(f32[1,512,4096]{1,2,0:T(8,128)} %copy.15, s32[512,4096]{0,1:T(8,128)} %copy.16), kind=kLoop, calls=%fused_computation.36 | loop fusion | flops 4194304 | bytes 25165824 | tf_op jit(solution)/shard_map/mul | solution.py:123
  29.3 17.6 %fusion.37 = f32[64,512,64]{1,0,2:T(8,128)} fusion(f32[512,64,64]{0,2,1:T(8,128)} %bitcast.90), kind=kOutput, calls=%fused_computation.67 | convolution fusion | flops 1610674176 | bytes 16777216 | tf_op jit(solution)/shard_map/yan,ak->ykn/dot_general | solution.py:53
  46.9 21.0 %subtract_bitcast_fusion.1 = (f32[512,64,64]{0,1,2:T(8,128)S(1)}, f32[512,64,64]{0,1,2:T(8,128)}) fusion(f32[64,512,64]{1,0,2:T(8,128)} %fusion.37, f32[64,64]{0,1:T(8,128)S(1)} %get-tuple-element.245, f32[64,64]{0,1:T(8,128)S(1)} %get-tuple-element.246, f32[512,64,64]{0,2,1:T(8,128)} %bitcast.91), kind=kOutput, calls=%fused_computation.42 | convolution fusion | flops 1623252992 | bytes 33587200 | tf_op jit(solution)/shard_map/yan,ak->ykn/dot_general | solution.py:52
  67.9 19.2 %fusion.29 = f32[64,512,64]{1,0,2:T(8,128)S(1)} fusion(f32[512,64,64]{0,1,2:T(8,128)} %get-tuple-element.240), kind=kOutput, calls=%fused_computation.59 | convolution fusion | flops 1610670080 | bytes 16777216 | tf_op jit(solution)/shard_map/ykn,nm->ymk/dot_general | solution.py:30
  87.1 13.9 %add_bitcast_fusion = f32[512,64,64]{0,1,2:T(8,128)} fusion(f32[64,512,64]{1,0,2:T(8,128)S(1)} %fusion.29, f32[512,64,64]{0,1,2:T(8,128)S(1)} %get-tuple-element.239), kind=kOutput, calls=%fused_computation.39 | convolution fusion | flops 1612771328 | bytes 25165824 | tf_op jit(solution)/shard_map/ykn,nm->ymk/dot_general | solution.py:30
  101.0 11.5 %copy.26 = f32[512,64,64]{0,2,1:T(8,128)} copy(f32[512,64,64]{0,1,2:T(8,128)} %add_bitcast_fusion) | data formatting | bytes 16777216 | tf_op jit(solution)/shard_map/add | solution.py:34
  117.9 16.3 %fusion.31 = f32[64,512,64]{1,0,2:T(8,128)S(1)} fusion(f32[512,64,64]{0,1,2:T(8,128)} %get-tuple-element.240), kind=kOutput, calls=%fused_computation.61 | convolution fusion | flops 1610674176 | bytes 16777216 | tf_op jit(solution)/shard_map/ykn,nm->ymk/dot_general | solution.py:30
  134.2 17.1 %subtract_bitcast_fusion = f32[512,64,64]{0,1,2:T(8,128)S(1)} fusion(f32[64,512,64]{1,0,2:T(8,128)S(1)} %fusion.31, f32[512,64,64]{0,1,2:T(8,128)} %copy-done), kind=kOutput, calls=%fused_computation.40 | convolution fusion | flops 1612767232 | bytes 25165824 | tf_op jit(solution)/shard_map/ykn,nm->ymk/dot_general | solution.py:30
  159.4 53.0 %all-to-all-done.1 = f32[512,8,512]{0,2,1:T(8,128)} async-done(((f32[512,8,512]{0,2,1:T(8,128)}), f32[512,8,512]{0,2,1:T(8,128)}, u32[]{:S(2)}, u32[]{:S(2)}) %all-to-all-start.1) | async-done | bytes 8388640 | tf_op jit(solution)/shard_map/all_to_all | solution.py:133
  226.9 17.8 %fusion.21 = f32[64,64,512]{2,0,1:T(8,128)} fusion(f32[64,64,512]{2,1,0:T(8,128)} %bitcast.92), kind=kOutput, calls=%fused_computation.51 | convolution fusion | flops 1610670080 | bytes 16777216 | tf_op jit(solution)/shard_map/anbc,ak->knbc/dot_general | solution.py:30
  244.7 13.8 %fusion.23 = f32[64,64,512]{2,0,1:T(8,128)} fusion(f32[64,64,512]{2,1,0:T(8,128)S(1)} %bitcast.93), kind=kOutput, calls=%fused_computation.53 | convolution fusion | flops 1610674176 | bytes 16777216 | tf_op jit(solution)/shard_map/anbc,ak->knbc/dot_general | solution.py:30
  258.5 53.4 %all-to-all-done = f32[512,8,512]{0,2,1:T(8,128)} async-done(((f32[512,8,512]{0,2,1:T(8,128)}), f32[512,8,512]{0,2,1:T(8,128)}, u32[]{:S(2)}, u32[]{:S(2)}) %all-to-all-start) | async-done | bytes 8388640 | tf_op jit(solution)/shard_map/all_to_all | solution.py:132
  311.8 9.2 copy.22
  321.0 17.7 %fusion.27 = f32[64,64,512]{2,0,1:T(8,128)} fusion(f32[64,64,512]{2,1,0:T(8,128)} %bitcast.94), kind=kOutput, calls=%fused_computation.57 | convolution fusion | flops 1610670080 | bytes 16777216 | tf_op jit(solution)/shard_map/anbc,ak->knbc/dot_general | solution.py:30
  338.7 24.6 %multiply_subtract_fusion = (f32[64,64,512]{2,0,1:T(8,128)}, f32[64,64,512]{2,0,1:T(8,128)}) fusion(f32[64,64]{0,1:T(8,128)S(1)} %get-tuple-element.245, f32[64,64]{0,1:T(8,128)S(1)} %get-tuple-element.246, f32[64,64,512]{2,0,1:T(8,128)} %fusion.21, f32[64,64,512]{2,0,1:T(8,128)} %fusion.27, f32[64,64,512]{2,0,1:T(8,128)} %fusion.23, ...), kind=kOutput, calls=%fused_computation.38 | convolution fusion | flops 1627451392 | bytes 50364416 | tf_op jit(solution)/shard_map/anbc,ak->knbc/dot_general | solution.py:30
  363.3 18.5 %fusion.13 = f32[64,64,512]{2,0,1:T(8,128)} fusion(f32[64,64,512]{2,0,1:T(8,128)} %get-tuple-element.238), kind=kOutput, calls=%fused_computation.43 | convolution fusion | flops 1610670080 | bytes 16777216 | tf_op jit(solution)/shard_map/knbc,nm->mkbc/dot_general | solution.py:30
  381.8 12.5 %fusion.15 = f32[64,64,512]{2,0,1:T(8,128)S(1)} fusion(f32[64,64,512]{2,0,1:T(8,128)S(1)} %copy-done.2), kind=kOutput, calls=%fused_computation.45 | convolution fusion | flops 1610674176 | bytes 16777216 | tf_op jit(solution)/shard_map/knbc,nm->mkbc/dot_general | solution.py:30
  394.3 15.6 %fusion.48 = f32[64,64,512]{2,0,1:T(8,128)} fusion(f32[64,64,512]{2,0,1:T(8,128)} %fusion.13, f32[64,64,512]{2,0,1:T(8,128)S(1)} %bitcast.89), kind=kOutput, calls=%fused_computation.76 | convolution fusion | flops 1612771328 | bytes 25165824 | tf_op jit(solution)/shard_map/knbc,nm->mkbc/dot_general | solution.py:30
  409.9 11.5 %copy.36 = f32[64,64,512]{2,1,0:T(8,128)} copy(f32[64,64,512]{2,0,1:T(8,128)} %fusion.48) | data formatting | bytes 16777216 | tf_op jit(solution)/shard_map/add | solution.py:34
  428.3 13.7 %fusion.45 = f32[64,64,512]{2,0,1:T(8,128)} fusion(f32[64,64,512]{2,0,1:T(8,128)S(1)} %fusion.15, f32[64,64,512]{2,0,1:T(8,128)S(1)} %bitcast.89), kind=kOutput, calls=%fused_computation.75 | convolution fusion | flops 1612767232 | bytes 25165824 | tf_op jit(solution)/shard_map/knbc,nm->mkbc/dot_general | solution.py:30
  460.7 59.4 %collective-permute-done.1 = f32[2048,512]{1,0:T(8,128)} collective-permute-done((f32[2048,512]{1,0:T(8,128)}, f32[2048,512]{1,0:T(8,128)}, u32[]{:S(2)}, u32[]{:S(2)}) %collective-permute-start.1) | collective-permute-done | bytes 4194336 | tf_op jit(solution)/shard_map/ppermute | solution.py:12
  528.2 78.0 %collective-permute-done = f32[2048,512]{1,0:T(8,128)} collective-permute-done((f32[2048,512]{1,0:T(8,128)}, f32[2048,512]{1,0:T(8,128)}, u32[]{:S(2)}, u32[]{:S(2)}) %collective-permute-start) | collective-permute-done | bytes 4194336 | tf_op jit(solution)/shard_map/ppermute | solution.py:12
  612.8 348.4 %while.14 = (s32[]{:T(128)}, f32[3,1024]{1,0:T(4,128)S(1)}, s32[]{:T(128)}, s32[8]{0:T(128)S(1)}, s32[]{:T(128)}, /*index=5*/f32[8,256,512]{2,1,0:T(8,128)}, f32...) while((s32[]{:T(128)}, f32[3,1024]{1,0:T(4,128)S(1)}, ...), condition=%wide.region_1.2_spmd.clone, body=%wide.region_0.1_spmd.clone.sunk | while | flops 832713472 | bytes 68505800 | solution.py:175
  622.1 28.9 %copy.81 = bf16[6,8,256,512]{3,1,2,0:T(8,128)(2,1)S(1)} copy(bf16[6,8,256,512]{3,2,1,0:T(8,128)(2,1)S(1)} %bitcast.86) | data formatting | bytes 25165824 | tf_op jit(solution)/shard_map/while
  665.6 28.9 %copy.81 = bf16[6,8,256,512]{3,1,2,0:T(8,128)(2,1)S(1)} copy(bf16[6,8,256,512]{3,2,1,0:T(8,128)(2,1)S(1)} %bitcast.86) | data formatting | bytes 25165824 | tf_op jit(solution)/shard_map/while
  709.2 28.9 %copy.81 = bf16[6,8,256,512]{3,1,2,0:T(8,128)(2,1)S(1)} copy(bf16[6,8,256,512]{3,2,1,0:T(8,128)(2,1)S(1)} %bitcast.86) | data formatting | bytes 25165824 | tf_op jit(solution)/shard_map/while
  752.7 28.9 %copy.81 = bf16[6,8,256,512]{3,1,2,0:T(8,128)(2,1)S(1)} copy(bf16[6,8,256,512]{3,2,1,0:T(8,128)(2,1)S(1)} %bitcast.86) | data formatting | bytes 25165824 | tf_op jit(solution)/shard_map/while
  796.2 28.9 %copy.81 = bf16[6,8,256,512]{3,1,2,0:T(8,128)(2,1)S(1)} copy(bf16[6,8,256,512]{3,2,1,0:T(8,128)(2,1)S(1)} %bitcast.86) | data formatting | bytes 25165824 | tf_op jit(solution)/shard_map/while
  839.7 28.9 %copy.81 = bf16[6,8,256,512]{3,1,2,0:T(8,128)(2,1)S(1)} copy(bf16[6,8,256,512]{3,2,1,0:T(8,128)(2,1)S(1)} %bitcast.86) | data formatting | bytes 25165824 | tf_op jit(solution)/shard_map/while
  883.3 28.9 %copy.81 = bf16[6,8,256,512]{3,1,2,0:T(8,128)(2,1)S(1)} copy(bf16[6,8,256,512]{3,2,1,0:T(8,128)(2,1)S(1)} %bitcast.86) | data formatting | bytes 25165824 | tf_op jit(solution)/shard_map/while
  926.8 28.9 %copy.81 = bf16[6,8,256,512]{3,1,2,0:T(8,128)(2,1)S(1)} copy(bf16[6,8,256,512]{3,2,1,0:T(8,128)(2,1)S(1)} %bitcast.86) | data formatting | bytes 25165824 | tf_op jit(solution)/shard_map/while
  961.3 41.8 %psum.7 = f32[2,3,1024]{2,0,1:T(2,128)S(1)} all-reduce(f32[2,3,1024]{2,0,1:T(2,128)S(1)} %broadcast_multiply_fusion.2), channel_id=1, replica_groups=mesh['rows'=8,'rep'=4] {'rows','rep'}, use_global_device_ids=true, to_apply=%region_2.3 | all-reduce | flops 6144 | bytes 49152 | tf_op jit(solution)/shard_map/psum | solution.py:182
  (152 shorter events, 198.2 us)
Async XLA Ops:
  67.9 19.2 %copy-start = (f32[512,64,64]{0,1,2:T(8,128)}, f32[512,64,64]{0,1,2:T(8,128)S(1)}, u32[]{:S(2)}) copy-start(f32[512,64,64]{0,1,2:T(8,128)S(1)} %get-tuple-element.239) | copy-start | bytes 25165828
  112.5 100.0 %all-to-all-start.1 = ((f32[512,8,512]{0,2,1:T(8,128)}), f32[512,8,512]{0,2,1:T(8,128)}, u32[]{:S(2)}, u32[]{:S(2)}) async-start(f32[512,8,512]{0,2,1:T(8,128)} %bitcast.103), calls=%async_computation.1 | async-start | bytes 16777216 | tf_op jit(solution)/shard_map/all_to_all | solution.py:133
  212.4 99.4 %all-to-all-start = ((f32[512,8,512]{0,2,1:T(8,128)}), f32[512,8,512]{0,2,1:T(8,128)}, u32[]{:S(2)}, u32[]{:S(2)}) async-start(f32[512,8,512]{0,2,1:T(8,128)} %bitcast.102), calls=%async_computation | async-start | bytes 16777216 | tf_op jit(solution)/shard_map/all_to_all | solution.py:132
  226.9 17.8 %copy-start.1 = (f32[8,512,1,512]{3,1,0,2:T(8,128)S(1)}, f32[8,512,1,512]{3,1,0,2:T(8,128)}, u32[]{:S(2)}) copy-start(f32[8,512,1,512]{3,1,0,2:T(8,128)} %copy.27) | copy-start | bytes 25165828
  363.3 18.5 %copy-start.2 = (f32[64,64,512]{2,0,1:T(8,128)S(1)}, f32[64,64,512]{2,0,1:T(8,128)}, u32[]{:S(2)}) copy-start(f32[64,64,512]{2,0,1:T(8,128)} %get-tuple-element.238) | copy-start | bytes 25165828
  363.3 31.0 %slice-start = ((s8[8388608]{0:T(1024)(128)(4,1)}), s8[4194304]{0:T(1024)(128)(4,1)S(1)}, s32[]{:S(2)}) async-start(s8[8388608]{0:T(1024)(128)(4,1)} %bitcast.88), calls=%async_computation.2 | async-start | bytes 8388608
  381.8 12.5 %slice-start.1 = ((s8[8388608]{0:T(1024)(128)(4,1)}), s8[4194304]{0:T(1024)(128)(4,1)S(1)}, s32[]{:S(2)}) async-start(s8[8388608]{0:T(1024)(128)(4,1)} %bitcast.88), calls=%async_computation.3 | async-start | bytes 8388608
  426.1 94.0 %collective-permute-start.1 = (f32[2048,512]{1,0:T(8,128)}, f32[2048,512]{1,0:T(8,128)}, u32[]{:S(2)}, u32[]{:S(2)}) collective-permute-start(f32[2048,512]{1,0:T(8,128)} %constant_dynamic-slice_fusion.1), channel_id=1, source_target_pairs={{0,1},{1,0},{2,3},{3,2},{4,5},{5,4},{6,7},{7,6},{8,9},{9,8},{10,11... | collective-permute-start | bytes 12582920 | tf_op jit(solution)/shard_map/ppermute | solution.py:12
  450.2 3.2 copy-start.3
  455.9 150.3 %collective-permute-start = (f32[2048,512]{1,0:T(8,128)}, f32[2048,512]{1,0:T(8,128)}, u32[]{:S(2)}, u32[]{:S(2)}) collective-permute-start(f32[2048,512]{1,0:T(8,128)} %constant_dynamic-slice_fusion.2), channel_id=1, source_target_pairs={{0,1},{1,0},{2,3},{3,2},{4,5},{5,4},{6,7},{7,6},{8,9},{9,8},{10,11... | collective-permute-start | bytes 12582920 | tf_op jit(solution)/shard_map/ppermute | solution.py:12
  455.9 150.3 %slice-start.2 = ((s8[8388608]{0:T(1024)(128)(4,1)}), s8[4194304]{0:T(1024)(128)(4,1)S(1)}, s32[]{:S(2)}) async-start(s8[8388608]{0:T(1024)(128)(4,1)} %bitcast.99), calls=%async_computation.4 | async-start | bytes 8388608
  460.7 145.5 %slice-start.3 = ((s8[8388608]{0:T(1024)(128)(4,1)}), s8[4194304]{0:T(1024)(128)(4,1)S(1)}, s32[]{:S(2)}) async-start(s8[8388608]{0:T(1024)(128)(4,1)} %bitcast.99), calls=%async_computation.5 | async-start | bytes 8388608
  612.8 390.4 %copy-start.4 = (f32[3]{0:T(128)S(1)}, f32[3]{0:T(128)}, u32[]{:S(2)}) copy-start(f32[3]{0:T(128)} %constant.195.clone) | copy-start | bytes 40
where the time goes:
time: 1010 us; the launch traced here: 1000 us
  local copies, waits for them, and re-layouts  329 us (33%)
  matrix products  282 us (28%)
  waiting for transfers between devices  244 us (24%)
  other arithmetic  87.5 us (9%)
  blocking collectives  41.8 us (4%)
  starting transfers between devices  13.1 us (1%)
    while x16, local copies, waits for them, and re-layouts  233 us
    dot_general x12, matrix products, product(): return jnp.einsum(form, left, right, precision=precise)  201 us
    ppermute x2, waiting for transfers between devices, partner(): lax.ppermute(array, axis, [(i, i ^ 1 << distance) for i in range(lax.axis...  137 us
    all_to_all x1, waiting for transfers between devices, on_device(): lax.all_to_all(slabs[0], 'rows', split_axis=1, concat_axis=0, tiled=True)  53.4 us
    all_to_all x1, waiting for transfers between devices, on_device(): lax.all_to_all(slabs[1], 'rows', split_axis=1, concat_axis=0, tiled=True)  53 us
    dot_general x8, matrix products, band_terms(): lax.dot_general(weighted, low_hot, (((1,), (1,)), ((), ())), preferred_el...  43.1 us
    psum x1, blocking collectives, on_device(): totals = lax.psum(slot * partial_sums[None], ('rows', 'rep'))  41.8 us
    add x2, local copies, waits for them, and re-layouts, complex_apply(): product(real_part, table_sin) + product(imag_part, table_cos)  23 us
  transfers between devices with their start and end apart: 4, of which 4 were waited for; matrix products, arithmetic and copies ran while one was open for 12% of the time, Pallas kernels for 0%

commit v1 on v0

--- a/solution.py
+++ b/solution.py
@@ -3,9 +3,26 @@
 import jax.numpy as jnp
 from jax import lax
 from jax.sharding import PartitionSpec as P
+from jax.lax import axis_index, axis_size, ppermute
 
 NBINS = 1024
 precise = lax.Precision.HIGHEST
+
+
+def _define_keys(arr_in, array_axis, piece_in):
+    e_next, a_next = (arr_in.shape[:array_axis], arr_in.shape[array_axis + 1 :])
+    all_rows = arr_in.reshape(*e_next, piece_in, -1, *a_next)
+    found_now = jnp.moveaxis(all_rows, array_axis, 0)
+    return found_now
+
+
+def plan_works(original, at_axis):
+    original = jnp.moveaxis(original, 0, at_axis)
+    formed = original.shape
+    mat_out = original.reshape(
+        *formed[:at_axis], formed[at_axis] * formed[at_axis + 1], *formed[at_axis + 2 :]
+    )
+    return mat_out
 
 
 def partner(array, axis, distance):
@@ -114,6 +131,24 @@
 
 
 def on_device(maps, mask, bins):
+
+    def hold_side_for(x0, arr, work_x, which_axis):
+        response = axis_size(which_axis)
+        y = axis_index(which_axis)
+        piece_now, e_now = (response, y)
+        side_arr = _define_keys(arr, x0, piece_now)
+        store = [side_arr[e_now]]
+        dev = 1
+        while dev < piece_now:
+            fresh = side_arr[e_now ^ dev]
+            p_next = ppermute(fresh, which_axis, [(t, t ^ dev) for t in range(piece_now)])
+            store.append(p_next)
+            dev = dev + 1
+        piece_out = jnp.stack(store, 0)
+        side_arr = piece_out[e_now ^ jnp.arange(piece_now)]
+        block_now = plan_works(side_arr, work_x)
+        return block_now
+
     extent = bins.shape[0]
     columns = bins.shape[1]
     count = maps.shape[1]
@@ -130,7 +165,7 @@
     spec_real, spec_imag = column_transform(
         (
             lax.all_to_all(slabs[0], "rows", split_axis=1, concat_axis=0, tiled=True),
-            lax.all_to_all(slabs[1], "rows", split_axis=1, concat_axis=0, tiled=True),
+            hold_side_for(1, slabs[1], 0, "rows"),
         )
     )
     spec_real = spec_real.reshape(extent, columns)

time: 1010 us -> 1050 us (1.040)
  local copies, waits for them, and re-layouts: 329 us -> 364 us
    ppermute x0 -> x7, waiting for transfers between devices: none -> 99.4 us  [hold_side_for(): ppermute(fresh, which_axis, [(t, t ^ dev) for t in range(piece_now)])]
    all_to_all x1, waiting for transfers between devices: 53.4 us -> 0.01 us  [on_device(): lax.all_to_all(slabs[0], 'rows', split_axis=1, concat_axis=0, tiled=True)]
    all_to_all x1 -> x0, waiting for transfers between devices: 53 us -> none  [on_device(): lax.all_to_all(slabs[1], 'rows', split_axis=1, concat_axis=0, tiled=True)]
    another operation x0 -> x10, local copies, waits for them, and re-layouts: none -> 23.1 us
    unnamed x20 -> x29, local copies, waits for them, and re-layouts: 21.3 us -> 35 us
  transfers between devices with their start and end apart: 4 -> 10, of which waited for: 4 -> 6; matrix products, arithmetic and copies ran while one was open for 12% -> 14% of each run, Pallas kernels for 0% -> 0%
where the time goes in v1:
time: 1050 us; the launch traced here: 1040 us
  local copies, waits for them, and re-layouts  364 us (35%)
  matrix products  282 us (27%)
  waiting for transfers between devices  240 us (23%)
  other arithmetic  87.6 us (8%)
  blocking collectives  39.9 us (4%)
  starting transfers between devices  15.2 us (1%)
    while x16, local copies, waits for them, and re-layouts  233 us
    dot_general x12, matrix products, product(): return jnp.einsum(form, left, right, precision=precise)  200 us
    ppermute x2, waiting for transfers between devices, partner(): lax.ppermute(array, axis, [(i, i ^ 1 << distance) for i in range(lax.axis...  141 us
    ppermute x7, waiting for transfers between devices, hold_side_for(): ppermute(fresh, which_axis, [(t, t ^ dev) for t in range(piece_now)])  99.4 us
    dot_general x8, matrix products, band_terms(): lax.dot_general(weighted, low_hot, (((1,), (1,)), ((), ())), preferred_el...  43.1 us
    psum x1, blocking collectives, on_device(): totals = lax.psum(slot * partial_sums[None], ('rows', 'rep'))  39.9 us
    unnamed x29, local copies, waits for them, and re-layouts  35 us
    another operation x9, local copies, waits for them, and re-layouts  22 us
  transfers between devices with their start and end apart: 10, of which 6 were waited for; matrix products, arithmetic and copies ran while one was open for 14% of the time, Pallas kernels for 0%

profile of v1, /device:TPU:0, one launch (start us, length us, event | category | flops | bytes accessed | tf_op | source)
XLA Modules:
  0.0 1036.3 jit_solution(7703362448789414446)
XLA Ops:
  29.3 17.6 %fusion.37 = f32[64,512,64]{1,0,2:T(8,128)} fusion(f32[512,64,64]{0,2,1:T(8,128)} %bitcast.113), kind=kOutput, calls=%fused_computation.68 | convolution fusion | flops 1610674176 | bytes 16777216 | tf_op jit(solution)/shard_map/yan,ak->ykn/dot_general | solution.py:70
  46.9 21.0 %subtract_bitcast_fusion.1 = (f32[512,64,64]{0,1,2:T(8,128)S(1)}, f32[512,64,64]{0,1,2:T(8,128)}) fusion(f32[64,512,64]{1,0,2:T(8,128)} %fusion.37, f32[64,64]{0,1:T(8,128)S(1)} %get-tuple-element.253, f32[64,64]{0,1:T(8,128)S(1)} %get-tuple-element.254, f32[512,64,64]{0,2,1:T(8,128)} %bitcast.114), kind=kOutput, calls=%fused_computation.43 | convolution fusion | flops 1623252992 | bytes 33587200 | tf_op jit(solution)/shard_map/yan,ak->ykn/dot_general | solution.py:69
  67.9 19.3 %fusion.31 = f32[64,512,64]{1,0,2:T(8,128)S(1)} fusion(f32[512,64,64]{0,1,2:T(8,128)} %get-tuple-element.240), kind=kOutput, calls=%fused_computation.62 | convolution fusion | flops 1610674176 | bytes 16777216 | tf_op jit(solution)/shard_map/ykn,nm->ymk/dot_general | solution.py:47
  87.2 13.7 %subtract_bitcast_fusion = f32[512,64,64]{0,1,2:T(8,128)} fusion(f32[64,512,64]{1,0,2:T(8,128)S(1)} %fusion.31, f32[512,64,64]{0,1,2:T(8,128)S(1)} %get-tuple-element.239), kind=kOutput, calls=%fused_computation.41 | convolution fusion | flops 1612767232 | bytes 25165824 | tf_op jit(solution)/shard_map/ykn,nm->ymk/dot_general | solution.py:47
  100.9 11.5 %copy.42 = f32[512,64,64]{0,2,1:T(8,128)} copy(f32[512,64,64]{0,1,2:T(8,128)} %subtract_bitcast_fusion) | data formatting | bytes 16777216 | tf_op jit(solution)/shard_map/sub | solution.py:50
  118.2 16.2 %fusion.29 = f32[64,512,64]{1,0,2:T(8,128)S(1)} fusion(f32[512,64,64]{0,1,2:T(8,128)} %get-tuple-element.240), kind=kOutput, calls=%fused_computation.60 | convolution fusion | flops 1610670080 | bytes 16777216 | tf_op jit(solution)/shard_map/ykn,nm->ymk/dot_general | solution.py:47
  134.4 17.1 %add_bitcast_fusion = f32[512,64,64]{0,1,2:T(8,128)S(1)} fusion(f32[64,512,64]{1,0,2:T(8,128)S(1)} %fusion.29, f32[512,64,64]{0,1,2:T(8,128)} %copy-done), kind=kOutput, calls=%fused_computation.40 | convolution fusion | flops 1612771328 | bytes 25165824 | tf_op jit(solution)/shard_map/ykn,nm->ymk/dot_general | solution.py:47
  192.1 42.9 %collective-permute-done.1 = f32[512,1,512]{2,0,1:T(8,128)} collective-permute-done((f32[512,1,512]{2,0,1:T(8,128)}, f32[512,1,512]{2,0,1:T(8,128)}, u32[]{:S(2)}, u32[]{:S(2)}) %collective-permute-start.1) | collective-permute-done | bytes 1048608 | tf_op jit(solution)/shard_map/ppermute | solution.py:144
  237.3 18.5 %collective-permute-done.2 = f32[512,1,512]{2,0,1:T(8,128)} collective-permute-done((f32[512,1,512]{2,0,1:T(8,128)}, f32[512,1,512]{2,0,1:T(8,128)}, u32[]{:S(2)}, u32[]{:S(2)}) %collective-permute-start.2) | collective-permute-done | bytes 1048608 | tf_op jit(solution)/shard_map/ppermute | solution.py:144
  262.6 18.1 %collective-permute-done.5 = f32[512,1,512]{2,0,1:T(8,128)S(1)} collective-permute-done((f32[512,1,512]{2,0,1:T(8,128)}, f32[512,1,512]{2,0,1:T(8,128)S(1)}, u32[]{:S(2)}, u32[]{:S(2)}) %collective-permute-start.5) | collective-permute-done | bytes 1048608 | tf_op jit(solution)/shard_map/ppermute | solution.py:144
  281.8 19.9 %collective-permute-done.6 = f32[512,1,512]{2,0,1:T(8,128)S(1)} collective-permute-done((f32[512,1,512]{2,0,1:T(8,128)S(1)}, f32[512,1,512]{2,0,1:T(8,128)S(1)}, u32[]{:S(2)}, u32[]{:S(2)}) %collective-permute-start.6) | collective-permute-done | bytes 1048608 | tf_op jit(solution)/shard_map/ppermute | solution.py:144
  310.5 17.8 %fusion.23 = f32[64,64,512]{2,0,1:T(8,128)} fusion(f32[64,64,512]{2,1,0:T(8,128)} %bitcast.117), kind=kOutput, calls=%fused_computation.54 | convolution fusion | flops 1610674176 | bytes 16777216 | tf_op jit(solution)/shard_map/anbc,ak->knbc/dot_general | solution.py:47
  337.5 18.2 %fusion.25 = f32[64,64,512]{2,0,1:T(8,128)} fusion(f32[64,64,512]{2,1,0:T(8,128)} %bitcast.115), kind=kOutput, calls=%fused_computation.56 | convolution fusion | flops 1610674176 | bytes 16777216 | tf_op jit(solution)/shard_map/anbc,ak->knbc/dot_general | solution.py:47
  355.7 13.3 %fusion.27 = f32[64,64,512]{2,0,1:T(8,128)} fusion(f32[64,64,512]{2,1,0:T(8,128)S(1)} %bitcast.116), kind=kOutput, calls=%fused_computation.58 | convolution fusion | flops 1610670080 | bytes 16777216 | tf_op jit(solution)/shard_map/anbc,ak->knbc/dot_general | solution.py:47
  369.0 24.6 %multiply_subtract_fusion = (f32[64,64,512]{2,0,1:T(8,128)}, f32[64,64,512]{2,0,1:T(8,128)}) fusion(f32[64,64]{0,1:T(8,128)S(1)} %get-tuple-element.253, f32[64,64]{0,1:T(8,128)S(1)} %get-tuple-element.254, f32[64,64,512]{2,0,1:T(8,128)} %fusion.25, f32[64,64,512]{2,0,1:T(8,128)} %fusion.27, f32[64,64,512]{2,0,1:T(8,128)} %fusion.23, ...), kind=kOutput, calls=%fused_computation.39 | convolution fusion | flops 1627447296 | bytes 50364416 | tf_op jit(solution)/shard_map/anbc,ak->knbc/dot_general | solution.py:47
  393.6 18.5 %fusion.13 = f32[64,64,512]{2,0,1:T(8,128)} fusion(f32[64,64,512]{2,0,1:T(8,128)} %get-tuple-element.238), kind=kOutput, calls=%fused_computation.44 | convolution fusion | flops 1610670080 | bytes 16777216 | tf_op jit(solution)/shard_map/knbc,nm->mkbc/dot_general | solution.py:47
  412.1 12.5 %fusion.15 = f32[64,64,512]{2,0,1:T(8,128)S(1)} fusion(f32[64,64,512]{2,0,1:T(8,128)S(1)} %copy-done.2), kind=kOutput, calls=%fused_computation.46 | convolution fusion | flops 1610674176 | bytes 16777216 | tf_op jit(solution)/shard_map/knbc,nm->mkbc/dot_general | solution.py:47
  424.6 15.6 %fusion.48 = f32[64,64,512]{2,0,1:T(8,128)} fusion(f32[64,64,512]{2,0,1:T(8,128)} %fusion.13, f32[64,64,512]{2,0,1:T(8,128)S(1)} %bitcast.112), kind=kOutput, calls=%fused_computation.77 | convolution fusion | flops 1612771328 | bytes 25165824 | tf_op jit(solution)/shard_map/knbc,nm->mkbc/dot_general | solution.py:47
  440.2 11.5 %copy.64 = f32[64,64,512]{2,1,0:T(8,128)} copy(f32[64,64,512]{2,0,1:T(8,128)} %fusion.48) | data formatting | bytes 16777216 | tf_op jit(solution)/shard_map/add | solution.py:51
  458.8 13.6 %fusion.45 = f32[64,64,512]{2,0,1:T(8,128)} fusion(f32[64,64,512]{2,0,1:T(8,128)S(1)} %fusion.15, f32[64,64,512]{2,0,1:T(8,128)S(1)} %bitcast.112), kind=kOutput, calls=%fused_computation.76 | convolution fusion | flops 1612767232 | bytes 25165824 | tf_op jit(solution)/shard_map/knbc,nm->mkbc/dot_general | solution.py:47
  491.2 59.4 %collective-permute-done.8 = f32[2048,512]{1,0:T(8,128)} collective-permute-done((f32[2048,512]{1,0:T(8,128)}, f32[2048,512]{1,0:T(8,128)}, u32[]{:S(2)}, u32[]{:S(2)}) %collective-permute-start.8) | collective-permute-done | bytes 4194336 | tf_op jit(solution)/shard_map/ppermute | solution.py:29
  558.7 81.4 %collective-permute-done.7 = f32[2048,512]{1,0:T(8,128)} collective-permute-done((f32[2048,512]{1,0:T(8,128)}, f32[2048,512]{1,0:T(8,128)}, u32[]{:S(2)}, u32[]{:S(2)}) %collective-permute-start.7) | collective-permute-done | bytes 4194336 | tf_op jit(solution)/shard_map/ppermute | solution.py:29
  646.8 348.4 %while.14 = (s32[]{:T(128)}, f32[3,1024]{1,0:T(4,128)S(1)}, s32[]{:T(128)}, s32[8]{0:T(128)S(1)}, s32[]{:T(128)}, /*index=5*/f32[8,256,512]{2,1,0:T(8,128)}, f32...) while((s32[]{:T(128)}, f32[3,1024]{1,0:T(4,128)S(1)}, ...), condition=%wide.region_1.2_spmd.clone, body=%wide.region_0.1_spmd.clone.sunk | while | flops 832713472 | bytes 68505800 | solution.py:210
  656.1 28.9 %copy.109 = bf16[6,8,256,512]{3,1,2,0:T(8,128)(2,1)S(1)} copy(bf16[6,8,256,512]{3,2,1,0:T(8,128)(2,1)S(1)} %bitcast.109) | data formatting | bytes 25165824 | tf_op jit(solution)/shard_map/while
  699.6 28.9 %copy.109 = bf16[6,8,256,512]{3,1,2,0:T(8,128)(2,1)S(1)} copy(bf16[6,8,256,512]{3,2,1,0:T(8,128)(2,1)S(1)} %bitcast.109) | data formatting | bytes 25165824 | tf_op jit(solution)/shard_map/while
  743.1 28.9 %copy.109 = bf16[6,8,256,512]{3,1,2,0:T(8,128)(2,1)S(1)} copy(bf16[6,8,256,512]{3,2,1,0:T(8,128)(2,1)S(1)} %bitcast.109) | data formatting | bytes 25165824 | tf_op jit(solution)/shard_map/while
  786.6 28.9 %copy.109 = bf16[6,8,256,512]{3,1,2,0:T(8,128)(2,1)S(1)} copy(bf16[6,8,256,512]{3,2,1,0:T(8,128)(2,1)S(1)} %bitcast.109) | data formatting | bytes 25165824 | tf_op jit(solution)/shard_map/while
  830.1 28.9 %copy.109 = bf16[6,8,256,512]{3,1,2,0:T(8,128)(2,1)S(1)} copy(bf16[6,8,256,512]{3,2,1,0:T(8,128)(2,1)S(1)} %bitcast.109) | data formatting | bytes 25165824 | tf_op jit(solution)/shard_map/while
  873.7 28.9 %copy.109 = bf16[6,8,256,512]{3,1,2,0:T(8,128)(2,1)S(1)} copy(bf16[6,8,256,512]{3,2,1,0:T(8,128)(2,1)S(1)} %bitcast.109) | data formatting | bytes 25165824 | tf_op jit(solution)/shard_map/while
  917.2 28.9 %copy.109 = bf16[6,8,256,512]{3,1,2,0:T(8,128)(2,1)S(1)} copy(bf16[6,8,256,512]{3,2,1,0:T(8,128)(2,1)S(1)} %bitcast.109) | data formatting | bytes 25165824 | tf_op jit(solution)/shard_map/while
  960.7 28.9 %copy.109 = bf16[6,8,256,512]{3,1,2,0:T(8,128)(2,1)S(1)} copy(bf16[6,8,256,512]{3,2,1,0:T(8,128)(2,1)S(1)} %bitcast.109) | data formatting | bytes 25165824 | tf_op jit(solution)/shard_map/while
  995.3 39.9 %psum.7 = f32[2,3,1024]{2,0,1:T(2,128)S(1)} all-reduce(f32[2,3,1024]{2,0,1:T(2,128)S(1)} %broadcast_multiply_fusion.2), channel_id=1, replica_groups=mesh['rows'=8,'rep'=4] {'rows','rep'}, use_global_device_ids=true, to_apply=%region_2.3 | all-reduce | flops 6144 | bytes 49152 | tf_op jit(solution)/shard_map/psum | solution.py:217
  (185 shorter events, 255.8 us)
Async XLA Ops:
  67.9 19.4 %copy-start = (f32[512,64,64]{0,1,2:T(8,128)}, f32[512,64,64]{0,1,2:T(8,128)S(1)}, u32[]{:S(2)}) copy-start(f32[512,64,64]{0,1,2:T(8,128)S(1)} %get-tuple-element.239) | copy-start | bytes 25165828
  112.4 216.0 %all-to-all-start = ((f32[512,8,512]{0,2,1:T(8,128)}), f32[512,8,512]{0,2,1:T(8,128)}, u32[]{:S(2)}, u32[]{:S(2)}) async-start(f32[512,8,512]{0,2,1:T(8,128)} %bitcast.120), calls=%async_computation | async-start | bytes 16777216 | tf_op jit(solution)/shard_map/all_to_all | solution.py:167
  168.5 18.8 %collective-permute-start = (f32[512,1,512]{2,0,1:T(8,128)}, f32[512,1,512]{2,0,1:T(8,128)}, u32[]{:S(2)}, u32[]{:S(2)}) collective-permute-start(f32[512,1,512]{2,0,1:T(8,128)} %bitcast.137), channel_id=1, source_target_pairs={{0,4},{4,0},{8,12},{12,8},{16,20},{20,16},{24,28},{28,24},{1,5},{5... | collective-permute-start | bytes 3145736 | tf_op jit(solution)/shard_map/ppermute | solution.py:144
  171.5 63.4 %collective-permute-start.1 = (f32[512,1,512]{2,0,1:T(8,128)}, f32[512,1,512]{2,0,1:T(8,128)}, u32[]{:S(2)}, u32[]{:S(2)}) collective-permute-start(f32[512,1,512]{2,0,1:T(8,128)} %bitcast.136), channel_id=1, source_target_pairs={{0,8},{4,12},{8,0},{12,4},{16,24},{20,28},{24,16},{28,20},{1,9},{5... | collective-permute-start | bytes 3145736 | tf_op jit(solution)/shard_map/ppermute | solution.py:144
  176.2 79.6 %collective-permute-start.2 = (f32[512,1,512]{2,0,1:T(8,128)}, f32[512,1,512]{2,0,1:T(8,128)}, u32[]{:S(2)}, u32[]{:S(2)}) collective-permute-start(f32[512,1,512]{2,0,1:T(8,128)} %bitcast.135), channel_id=1, source_target_pairs={{0,12},{4,8},{8,4},{12,0},{16,28},{20,24},{24,20},{28,16},{1,13},{... | collective-permute-start | bytes 3145736 | tf_op jit(solution)/shard_map/ppermute | solution.py:144
  178.8 79.2 %collective-permute-start.3 = (f32[512,1,512]{2,0,1:T(8,128)}, f32[512,1,512]{2,0,1:T(8,128)}, u32[]{:S(2)}, u32[]{:S(2)}) collective-permute-start(f32[512,1,512]{2,0,1:T(8,128)} %bitcast.134), channel_id=1, source_target_pairs={{0,16},{4,20},{8,24},{12,28},{16,0},{20,4},{24,8},{28,12},{1,17},{... | collective-permute-start | bytes 3145736 | tf_op jit(solution)/shard_map/ppermute | solution.py:144
  183.1 77.2 %collective-permute-start.4 = (f32[512,1,512]{2,0,1:T(8,128)}, f32[512,1,512]{2,0,1:T(8,128)}, u32[]{:S(2)}, u32[]{:S(2)}) collective-permute-start(f32[512,1,512]{2,0,1:T(8,128)} %bitcast.133), channel_id=1, source_target_pairs={{0,20},{4,16},{8,28},{12,24},{16,4},{20,0},{24,12},{28,8},{1,21},{... | collective-permute-start | bytes 3145736 | tf_op jit(solution)/shard_map/ppermute | solution.py:144
  184.5 50.5 %copy-start.4 = (f32[512,1,1,512]{3,0,2,1:T(8,128)S(1)}, f32[512,1,1,512]{3,0,2,1:T(8,128)}, u32[]{:S(2)}) copy-start(f32[512,1,1,512]{3,0,2,1:T(8,128)} %copy.55) | copy-start | bytes 3145732
  187.3 93.4 %collective-permute-start.5 = (f32[512,1,512]{2,0,1:T(8,128)}, f32[512,1,512]{2,0,1:T(8,128)S(1)}, u32[]{:S(2)}, u32[]{:S(2)}) collective-permute-start(f32[512,1,512]{2,0,1:T(8,128)} %bitcast.139), channel_id=1, source_target_pairs={{0,24},{4,28},{8,16},{12,20},{16,8},{20,12},{24,0},{28,4},{1,25},{... | collective-permute-start | bytes 3145736 | tf_op jit(solution)/shard_map/ppermute | solution.py:144
  235.0 66.8 %collective-permute-start.6 = (f32[512,1,512]{2,0,1:T(8,128)S(1)}, f32[512,1,512]{2,0,1:T(8,128)S(1)}, u32[]{:S(2)}, u32[]{:S(2)}) collective-permute-start(f32[512,1,512]{2,0,1:T(8,128)S(1)} %bitcast.138), channel_id=1, source_target_pairs={{0,28},{4,24},{8,20},{12,16},{16,12},{20,8},{24,4},{28,0},{1,29},{... | collective-permute-start | bytes 3145736 | tf_op jit(solution)/shard_map/ppermute | solution.py:144
  337.5 18.2 %copy-start.1 = (f32[8,512,1,512]{3,1,0,2:T(8,128)S(1)}, f32[8,512,1,512]{3,1,0,2:T(8,128)}, u32[]{:S(2)}) copy-start(f32[8,512,1,512]{3,1,0,2:T(8,128)} %copy.43) | copy-start | bytes 25165828
  393.6 18.5 %copy-start.2 = (f32[64,64,512]{2,0,1:T(8,128)S(1)}, f32[64,64,512]{2,0,1:T(8,128)}, u32[]{:S(2)}) copy-start(f32[64,64,512]{2,0,1:T(8,128)} %get-tuple-element.238) | copy-start | bytes 25165828
  393.6 31.0 %slice-start = ((s8[8388608]{0:T(1024)(128)(4,1)}), s8[4194304]{0:T(1024)(128)(4,1)S(1)}, s32[]{:S(2)}) async-start(s8[8388608]{0:T(1024)(128)(4,1)} %bitcast.111), calls=%async_computation.1 | async-start | bytes 8388608
  412.1 12.5 %slice-start.1 = ((s8[8388608]{0:T(1024)(128)(4,1)}), s8[4194304]{0:T(1024)(128)(4,1)S(1)}, s32[]{:S(2)}) async-start(s8[8388608]{0:T(1024)(128)(4,1)} %bitcast.111), calls=%async_computation.2 | async-start | bytes 8388608
  456.4 94.2 %collective-permute-start.8 = (f32[2048,512]{1,0:T(8,128)}, f32[2048,512]{1,0:T(8,128)}, u32[]{:S(2)}, u32[]{:S(2)}) collective-permute-start(f32[2048,512]{1,0:T(8,128)} %constant_dynamic-slice_fusion.1), channel_id=1, source_target_pairs={{0,1},{1,0},{2,3},{3,2},{4,5},{5,4},{6,7},{7,6},{8,9},{9,8},{10,11... | collective-permute-start | bytes 12582920 | tf_op jit(solution)/shard_map/ppermute | solution.py:29
  480.7 3.2 copy-start.3
  486.4 153.8 %collective-permute-start.7 = (f32[2048,512]{1,0:T(8,128)}, f32[2048,512]{1,0:T(8,128)}, u32[]{:S(2)}, u32[]{:S(2)}) collective-permute-start(f32[2048,512]{1,0:T(8,128)} %constant_dynamic-slice_fusion.2), channel_id=1, source_target_pairs={{0,1},{1,0},{2,3},{3,2},{4,5},{5,4},{6,7},{7,6},{8,9},{9,8},{10,11... | collective-permute-start | bytes 12582920 | tf_op jit(solution)/shard_map/ppermute | solution.py:29
  486.4 153.7 %slice-start.2 = ((s8[8388608]{0:T(1024)(128)(4,1)}), s8[4194304]{0:T(1024)(128)(4,1)S(1)}, s32[]{:S(2)}) async-start(s8[8388608]{0:T(1024)(128)(4,1)} %bitcast.124), calls=%async_computation.3 | async-start | bytes 8388608
  491.2 149.0 %slice-start.3 = ((s8[8388608]{0:T(1024)(128)(4,1)}), s8[4194304]{0:T(1024)(128)(4,1)S(1)}, s32[]{:S(2)}) async-start(s8[8388608]{0:T(1024)(128)(4,1)} %bitcast.124), calls=%async_computation.4 | async-start | bytes 8388608
  646.8 388.3 %copy-start.5 = (f32[3]{0:T(128)S(1)}, f32[3]{0:T(128)}, u32[]{:S(2)}) copy-start(f32[3]{0:T(128)} %constant.209.clone) | copy-start | bytes 40
